TPU v7x, 32 devices: a whole 2x2x4 slice. The times are simulated.
32 devices in a mesh: task: 4 (over x, core), param: 8 (over z, y).
Axes of the slice: x: 2, y: 2, z: 4, core: 2. Of those that a mesh axis runs over, the one named last changes fastest.
Arguments:
- acts: bfloat16 [128, 3584], replicated, may hold values from -6 to 6
- out_grads: bfloat16 [4, 128, 10240], P('task', None, 'param'), may hold values from -12 to 12
- order: int32 [4], replicated, may hold values from 0 to 3, each once
Outputs:
- update: float32 [3584, 10240], P('task', 'param')
- weights: float32 [4], replicated
All inputs are finite; a program needn't handle non-finite values.
Results may differ from a plain program's by a relative error of at most 0.0029.
Values may be sent and summed in bfloat16 or wider, within the bound.
A program may use at most 64 MiB of HBM per device.

v0:
```python
import jax
import jax.numpy as jnp
from jax import lax
from jax.sharding import PartitionSpec as P


def task_grads(acts_part, blocks):
    return jnp.einsum("td,ktc->kdc", acts_part, blocks, preferred_element_type=jnp.float32).astype(
        jnp.bfloat16
    )


def pcgrad_weights(gram, order):
    count = gram.shape[0]
    ids = jnp.arange(count, dtype=jnp.int32)

    def turn(step, mix):
        target = order[step]
        column = gram[:, target]
        onehot = (ids == target).astype(jnp.float32)
        dots = jnp.dot(mix, column, precision=lax.Precision.HIGHEST)
        scale = jnp.sum(column * onehot) + 1e-06
        change = jnp.minimum(dots, 0.0) / scale * (1.0 - onehot)
        return mix - change[:, None] * onehot[None, :]

    mix = lax.fori_loop(0, count, turn, jnp.eye(count, dtype=jnp.float32))
    return jnp.sum(mix, axis=0)


def shards(acts, out_grads, order):
    local = out_grads.shape[0]
    groups = lax.axis_size("task")
    group_id = lax.axis_index("task")
    total_tasks = local * groups
    part_rows = acts.shape[1] // groups
    acts_rows = lax.dynamic_slice_in_dim(acts, group_id * part_rows, part_rows, 1)
    everyone = lax.all_gather(out_grads, "task", axis=0, tiled=True)
    row_grads = task_grads(acts_rows, everyone)
    flat = row_grads.reshape(total_tasks, -1)
    partial_gram = jnp.dot(flat, flat.T, preferred_element_type=jnp.float32)
    gram = lax.psum(partial_gram, ("task", "param"))
    weights = pcgrad_weights(gram, order)
    combined = jnp.einsum(
        "k,ktc->tc", weights, everyone.astype(jnp.float32), precision=lax.Precision.HIGHEST
    ).astype(jnp.bfloat16)
    update = lax.dot_general(
        acts_rows, combined, (((0,), (0,)), ((), ())), preferred_element_type=jnp.float32
    )
    return (update, weights)


def solution(mesh):
    in_specs = (P(), P("task", None, "param"), P())
    out_specs = (P("task", "param"), P())
    return jax.shard_map(shards, mesh=mesh, in_specs=in_specs, out_specs=out_specs, check_vma=False)
```

profile of v0, /device:TPU:0, one launch (start us, length us, event | category | flops | bytes accessed | tf_op | source)
XLA Modules:
  0.0 130.1 jit_solution(3699769488526502229)
XLA Ops:
  7.2 0.7 all-gather.2.cloned.1.call-update
  7.9 22.5 %all-gather.2.cloned.1.call-done = bf16[4,128,1280]{2,1,0:T(8,128)(2,1)} async-done(((bf16[1,128,1280]{2,1,0:T(8,128)(2,1)}), bf16[4,128,1280]{2,1,0:T(8,128)(2,1)}) %all-gather.2.cloned.1.call-update) | async-done | bytes 1310736 | tf_op jit(solution)/shard_map/all_gather | solution.py:37
  30.5 3.9 %convolution_convert_fusion = bf16[896,4,1280]{2,0,1:T(8,128)(2,1)S(1)} fusion(bf16[4,128,1280]{2,1,0:T(8,128)(2,1)} %all-gather.2.cloned.1.call-done, bf16[128,3584]{1,0:T(8,128)(2,1)S(1)} %copy-done, s32[]{:T(128)S(6)} %select_n.15), kind=kOutput, calls=%fused_computation.10 | convolution fusion | flops 1178992640 | bytes 10715140 | tf_op jit(solution)/shard_map/td,ktc->kdc/dot_general | solution.py:8
  34.4 20.1 %fusion.9 = f32[4,4]{1,0:T(4,128)S(1)} fusion(bf16[896,4,1280]{2,0,1:T(8,128)(2,1)S(1)} %convolution_convert_fusion), kind=kOutput, calls=%fused_computation.15 | convolution fusion | flops 36700160 | bytes 9175104 | tf_op jit(solution)/shard_map/dot_general | solution.py:40
  54.4 39.3 %psum.7 = f32[4,4]{1,0:T(4,128)S(1)} all-reduce(f32[4,4]{1,0:T(4,128)S(1)} %fusion.9), channel_id=1, replica_groups=mesh['task'=4,'param'=8] {'task','param'}, use_global_device_ids=true, to_apply=%region_0.0 | all-reduce | flops 16 | bytes 128 | tf_op jit(solution)/shard_map/psum | solution.py:41
  93.8 23.9 %while.14 = (s32[]{:T(128)}, f32[4,4]{1,0:T(4,128)S(1)}, s32[4]{0:T(128)S(1)}, f32[4,4]{0,1:T(4,128)S(1)}, s32[]{:T(128)}, /*index=5*/s32[]{:T(128)}, s32[]{:T(128)}, f32[]{:T(128)}) while((s32[]{:T(128)}, f32[4,4]{1,0:T(4,128)S(1)}, s32[4]{0:T(128)S(1)}, f32[4,4]{0,1:T(4,128)S(1)}, s32[]{:T(128)}, /*index=5*/s32[]{:T(128)}, ...), condition=%wide.region_3.0_spmd.clone, body=%wide.region_1.0_spmd.clone.sunk | while | flops 273 | bytes 2939 | solution.py:26
  93.8 0.6 dynamic_slice.35
  96.4 1.3 fusion.24
  98.3 0.8 fusion.25
  99.1 0.7 compare_convert_fusion.2
  99.8 0.6 dynamic_slice.35
  102.3 1.3 fusion.24
  104.3 0.8 fusion.25
  105.0 0.7 compare_convert_fusion.2
  105.8 0.6 dynamic_slice.35
  108.3 1.3 fusion.24
  110.2 0.8 fusion.25
  111.0 0.7 compare_convert_fusion.2
  111.7 0.6 dynamic_slice.35
  114.3 1.3 fusion.24
  116.2 0.8 fusion.25
  117.0 0.7 compare_convert_fusion.2
  117.7 2.5 %fusion.7 = bf16[1,128,1280]{2,0,1:T(2,128)(2,1)S(1)} fusion(bf16[4,128,1280]{2,1,0:T(8,128)(2,1)S(1)} %copy-done.1, f32[4]{0:T(128)S(1)} %reduce_sum.22), kind=kOutput, calls=%fused_computation.13 | convolution fusion | flops 7864320 | bytes 1638416 | tf_op jit(solution)/shard_map/k,ktc->tc/dot_general | solution.py:43
  120.3 2.9 %fusion.10 = f32[896,1280]{1,0:T(8,128)} fusion(bf16[1,128,1280]{2,0,1:T(2,128)(2,1)S(1)} %fusion.7, bf16[128,3584]{1,0:T(8,128)(2,1)S(1)} %copy-done, s32[]{:T(128)S(6)} %select_n.15), kind=kOutput, calls=%fused_computation.17 | convolution fusion | flops 293601280 | bytes 5472260 | tf_op jit(solution)/shard_map/dot_general | solution.py:46
  (16 shorter events, 0.5 us)
Async XLA Ops:
  7.2 23.3 %copy-start = (bf16[128,3584]{1,0:T(8,128)(2,1)S(1)}, bf16[128,3584]{1,0:T(8,128)(2,1)}, u32[]{:S(2)}) copy-start(bf16[128,3584]{1,0:T(8,128)(2,1)} %param.5) | copy-start | bytes 2752516
  7.2 23.3 %all-gather.2.cloned.1.call-start = ((), (), s32[]{:S(2)}) async-start(), calls=%async_computation | async-start | bytes 1638400 | tf_op jit(solution)/shard_map/all_gather | solution.py:37
  34.4 59.5 %copy-start.3 = (s32[4]{0:T(128)S(1)}, s32[4]{0:T(128)}, u32[]{:S(2)}) copy-start(s32[4]{0:T(128)} %param.7) | copy-start | bytes 52
  34.4 83.4 %copy-start.1 = (bf16[4,128,1280]{2,1,0:T(8,128)(2,1)S(1)}, bf16[4,128,1280]{2,1,0:T(8,128)(2,1)}, u32[]{:S(2)}) copy-start(bf16[4,128,1280]{2,1,0:T(8,128)(2,1)} %all-gather.2.cloned.1.call-done) | copy-start | bytes 3932164
  117.7 5.5 %copy-start.2 = (f32[4]{0:T(128)}, f32[4]{0:T(128)S(1)}, u32[]{:S(2)}) copy-start(f32[4]{0:T(128)S(1)} %reduce_sum.22) | copy-start | bytes 52
Sparse Core Ops, SparseCore 0:
  9.5 20.8 all-gather.1
where the time goes:
time: 131 us; the launch traced here: 130 us
  blocking collectives  39.3 us (30%)
  matrix products  32.5 us (25%)
  waiting for transfers between devices  23.2 us (18%)
  between operations  14.1 us (11%)
  loops' own time  10.4 us (8%)
  other arithmetic  8.09 us (6%)
  local copies, waits for them, and re-layouts  2.45 us (2%)
    psum x1, blocking collectives, shards(): gram = lax.psum(partial_gram, ('task', 'param'))  39.3 us
    all_gather x1, waiting for transfers between devices, shards(): everyone = lax.all_gather(out_grads, 'task', axis=0, tiled=True)  22.5 us
    dot_general x1, matrix products, shards(): partial_gram = jnp.dot(flat, flat.T, preferred_element_type=jnp.float32)  20.1 us
    another operation x1, loops' own time, pcgrad_weights(): mix = lax.fori_loop(0, count, turn, jnp.eye(count, dtype=jnp.float32))  10.4 us
    reduce_sum x4, other arithmetic, turn(): scale = jnp.sum(column * onehot) + 1e-06  5.13 us
    dot_general x1, matrix products, task_grads(): jnp.einsum('td,ktc->kdc', acts_part, blocks, preferred_element_type=jnp.f...  3.88 us
    dot_general x4, matrix products, turn(): dots = jnp.dot(mix, column, precision=lax.Precision.HIGHEST)  3.12 us
    dot_general x1, matrix products, shards(): lax.dot_general(acts_rows, combined, (((0,), (0,)), ((), ())), preferred_...  2.94 us
  transfers between devices with their start and end apart: 1, of which 1 were waited for; matrix products, arithmetic and copies ran while one was open for 0% of the time, Pallas kernels for 0%

commit v1 on v0

--- a/solution.py
+++ b/solution.py
@@ -38,7 +38,8 @@
     row_grads = task_grads(acts_rows, everyone)
     flat = row_grads.reshape(total_tasks, -1)
     partial_gram = jnp.dot(flat, flat.T, preferred_element_type=jnp.float32)
-    gram = lax.psum(partial_gram, ("task", "param"))
+    half = lax.psum(partial_gram, "param")
+    gram = lax.psum(half, "task")
     weights = pcgrad_weights(gram, order)
     combined = jnp.einsum(
         "k,ktc->tc", weights, everyone.astype(jnp.float32), precision=lax.Precision.HIGHEST

time: 131 us -> 118 us (0.901)
  blocking collectives: 39.3 us -> 27.3 us
    psum x1 -> x2, blocking collectives: 39.3 us -> 27.3 us  [the longest x1 21.4 us: shards(): half = lax.psum(partial_gram, 'param')]
where the time goes in v1:
time: 118 us
  matrix products  32.5 us (28%)
  blocking collectives  27.3 us (23%)
  waiting for transfers between devices  23.2 us (20%)
  between operations  14.1 us (12%)
  loops' own time  10.4 us (9%)
  other arithmetic  8.09 us (7%)
  local copies, waits for them, and re-layouts  2.45 us (2%)
    all_gather x1, waiting for transfers between devices, shards(): everyone = lax.all_gather(out_grads, 'task', axis=0, tiled=True)  22.5 us
    psum x1, blocking collectives, shards(): half = lax.psum(partial_gram, 'param')  21.4 us
    dot_general x1, matrix products, shards(): partial_gram = jnp.dot(flat, flat.T, preferred_element_type=jnp.float32)  20.1 us
    another operation x1, loops' own time, pcgrad_weights(): mix = lax.fori_loop(0, count, turn, jnp.eye(count, dtype=jnp.float32))  10.4 us
    psum x1, blocking collectives, shards(): gram = lax.psum(half, 'task')  5.95 us
    reduce_sum x4, other arithmetic, turn(): scale = jnp.sum(column * onehot) + 1e-06  5.13 us
    dot_general x1, matrix products, task_grads(): jnp.einsum('td,ktc->kdc', acts_part, blocks, preferred_element_type=jnp.f...  3.88 us
    dot_general x4, matrix products, turn(): dots = jnp.dot(mix, column, precision=lax.Precision.HIGHEST)  3.12 us
  transfers between devices with their start and end apart: 1, of which 1 were waited for; matrix products, arithmetic and copies ran while one was open for 0% of the time, Pallas kernels for 0%

profile of v1, /device:TPU:0, one launch (start us, length us, event | category | flops | bytes accessed | tf_op | source)
XLA Modules:
  0.0 118.1 jit_solution(1607498618588159147)
XLA Ops:
  7.2 0.7 all-gather.2.cloned.1.call-update
  7.9 22.5 %all-gather.2.cloned.1.call-done = bf16[4,128,1280]{2,1,0:T(8,128)(2,1)} async-done(((bf16[1,128,1280]{2,1,0:T(8,128)(2,1)}), bf16[4,128,1280]{2,1,0:T(8,128)(2,1)}) %all-gather.2.cloned.1.call-update) | async-done | bytes 1310736 | tf_op jit(solution)/shard_map/all_gather | solution.py:37
  30.5 3.9 %convolution_convert_fusion = bf16[896,4,1280]{2,0,1:T(8,128)(2,1)S(1)} fusion(bf16[4,128,1280]{2,1,0:T(8,128)(2,1)} %all-gather.2.cloned.1.call-done, bf16[128,3584]{1,0:T(8,128)(2,1)S(1)} %copy-done, s32[]{:T(128)S(6)} %select_n.15), kind=kOutput, calls=%fused_computation.10 | convolution fusion | flops 1178992640 | bytes 10715140 | tf_op jit(solution)/shard_map/td,ktc->kdc/dot_general | solution.py:8
  34.4 20.1 %fusion.9 = f32[4,4]{1,0:T(4,128)S(1)} fusion(bf16[896,4,1280]{2,0,1:T(8,128)(2,1)S(1)} %convolution_convert_fusion), kind=kOutput, calls=%fused_computation.15 | convolution fusion | flops 36700160 | bytes 9175104 | tf_op jit(solution)/shard_map/dot_general | solution.py:40
  54.4 21.4 %psum.14 = f32[4,4]{1,0:T(4,128)S(1)} all-reduce(f32[4,4]{1,0:T(4,128)S(1)} %fusion.9), channel_id=1, replica_groups=mesh['task'=4,'param'=8] {'param'}, use_global_device_ids=true, to_apply=%region_0.0 | all-reduce | flops 16 | bytes 128 | tf_op jit(solution)/shard_map/psum | solution.py:41
  75.8 5.9 %psum.15 = f32[4,4]{1,0:T(4,128)S(1)} all-reduce(f32[4,4]{1,0:T(4,128)S(1)} %psum.14), channel_id=1, replica_groups=mesh['task'=4,'param'=8] {'task'}, use_global_device_ids=true, to_apply=%region_1.0 | all-reduce | flops 16 | bytes 128 | tf_op jit(solution)/shard_map/psum | solution.py:42
  81.8 23.9 %while.14 = (s32[]{:T(128)}, f32[4,4]{1,0:T(4,128)S(1)}, s32[4]{0:T(128)S(1)}, f32[4,4]{0,1:T(4,128)S(1)}, s32[]{:T(128)}, /*index=5*/s32[]{:T(128)}, s32[]{:T(128)}, f32[]{:T(128)}) while((s32[]{:T(128)}, f32[4,4]{1,0:T(4,128)S(1)}, s32[4]{0:T(128)S(1)}, f32[4,4]{0,1:T(4,128)S(1)}, s32[]{:T(128)}, /*index=5*/s32[]{:T(128)}, ...), condition=%wide.region_4.0_spmd.clone, body=%wide.region_2.0_spmd.clone.sunk | while | flops 273 | bytes 2939 | solution.py:26
  81.8 0.6 dynamic_slice.35
  84.4 1.3 %fusion.24 = f32[]{:T(128)} fusion(s32[]{:T(128)} %bitcast.36, f32[4,4]{0,1:T(4,128)S(1)} %get-tuple-element.167, s32[]{:T(128)S(6)} %select_n.18), kind=kLoop, calls=%fused_computation.8.clone.1 | loop fusion | flops 11 | bytes 28 | tf_op jit(solution)/shard_map/while/body/eval_jaxpr/reduce_sum | solution.py:22
  86.3 0.8 fusion.25
  87.1 0.7 compare_convert_fusion.2
  87.8 0.6 dynamic_slice.35
  90.3 1.3 %fusion.24 = f32[]{:T(128)} fusion(s32[]{:T(128)} %bitcast.36, f32[4,4]{0,1:T(4,128)S(1)} %get-tuple-element.167, s32[]{:T(128)S(6)} %select_n.18), kind=kLoop, calls=%fused_computation.8.clone.1 | loop fusion | flops 11 | bytes 28 | tf_op jit(solution)/shard_map/while/body/eval_jaxpr/reduce_sum | solution.py:22
  92.2 0.8 fusion.25
  93.0 0.7 compare_convert_fusion.2
  93.8 0.6 dynamic_slice.35
  96.3 1.3 %fusion.24 = f32[]{:T(128)} fusion(s32[]{:T(128)} %bitcast.36, f32[4,4]{0,1:T(4,128)S(1)} %get-tuple-element.167, s32[]{:T(128)S(6)} %select_n.18), kind=kLoop, calls=%fused_computation.8.clone.1 | loop fusion | flops 11 | bytes 28 | tf_op jit(solution)/shard_map/while/body/eval_jaxpr/reduce_sum | solution.py:22
  98.2 0.8 fusion.25
  99.0 0.7 compare_convert_fusion.2
  102.3 1.3 %fusion.24 = f32[]{:T(128)} fusion(s32[]{:T(128)} %bitcast.36, f32[4,4]{0,1:T(4,128)S(1)} %get-tuple-element.167, s32[]{:T(128)S(6)} %select_n.18), kind=kLoop, calls=%fused_computation.8.clone.1 | loop fusion | flops 11 | bytes 28 | tf_op jit(solution)/shard_map/while/body/eval_jaxpr/reduce_sum | solution.py:22
  104.2 0.8 fusion.25
  105.0 0.7 compare_convert_fusion.2
  105.7 2.5 %fusion.7 = bf16[1,128,1280]{2,0,1:T(2,128)(2,1)S(1)} fusion(bf16[4,128,1280]{2,1,0:T(8,128)(2,1)S(1)} %copy-done.1, f32[4]{0:T(128)S(1)} %reduce_sum.22), kind=kOutput, calls=%fused_computation.13 | convolution fusion | flops 7864320 | bytes 1638416 | tf_op jit(solution)/shard_map/k,ktc->tc/dot_general | solution.py:44
  108.3 2.9 %fusion.10 = f32[896,1280]{1,0:T(8,128)} fusion(bf16[1,128,1280]{2,0,1:T(2,128)(2,1)S(1)} %fusion.7, bf16[128,3584]{1,0:T(8,128)(2,1)S(1)} %copy-done, s32[]{:T(128)S(6)} %select_n.15), kind=kOutput, calls=%fused_computation.17 | convolution fusion | flops 293601280 | bytes 5472260 | tf_op jit(solution)/shard_map/dot_general | solution.py:47
  (17 shorter events, 1.1 us)
Async XLA Ops:
  7.2 23.3 %copy-start = (bf16[128,3584]{1,0:T(8,128)(2,1)S(1)}, bf16[128,3584]{1,0:T(8,128)(2,1)}, u32[]{:S(2)}) copy-start(bf16[128,3584]{1,0:T(8,128)(2,1)} %param.5) | copy-start | bytes 2752516
  7.2 23.3 %all-gather.2.cloned.1.call-start = ((), (), s32[]{:S(2)}) async-start(), calls=%async_computation | async-start | bytes 1638400 | tf_op jit(solution)/shard_map/all_gather | solution.py:37
  34.4 47.5 %copy-start.3 = (s32[4]{0:T(128)S(1)}, s32[4]{0:T(128)}, u32[]{:S(2)}) copy-start(s32[4]{0:T(128)} %param.7) | copy-start | bytes 52
  34.4 71.4 %copy-start.1 = (bf16[4,128,1280]{2,1,0:T(8,128)(2,1)S(1)}, bf16[4,128,1280]{2,1,0:T(8,128)(2,1)}, u32[]{:S(2)}) copy-start(bf16[4,128,1280]{2,1,0:T(8,128)(2,1)} %all-gather.2.cloned.1.call-done) | copy-start | bytes 3932164
  105.7 5.5 %copy-start.2 = (f32[4]{0:T(128)}, f32[4]{0:T(128)S(1)}, u32[]{:S(2)}) copy-start(f32[4]{0:T(128)S(1)} %reduce_sum.22) | copy-start | bytes 52
Sparse Core Ops, SparseCore 0:
  9.5 20.8 all-gather.1

commit v2 on v0

--- a/solution.py
+++ b/solution.py
@@ -38,7 +38,7 @@
     row_grads = task_grads(acts_rows, everyone)
     flat = row_grads.reshape(total_tasks, -1)
     partial_gram = jnp.dot(flat, flat.T, preferred_element_type=jnp.float32)
-    gram = lax.psum(partial_gram, ("task", "param"))
+    gram = lax.all_gather(partial_gram, ("task", "param")).sum(axis=0)
     weights = pcgrad_weights(gram, order)
     combined = jnp.einsum(
         "k,ktc->tc", weights, everyone.astype(jnp.float32), precision=lax.Precision.HIGHEST

time: 131 us -> 159 us (1.21)
  blocking collectives: 39.3 us -> 67.7 us
    all_gather x0 -> x1, blocking collectives: none -> 67.7 us  [shards(): gram = lax.all_gather(partial_gram, ('task', 'param')).sum(axis=0)]
    psum x1 -> x0, blocking collectives: 39.3 us -> none  [shards(): gram = lax.psum(partial_gram, ('task', 'param'))]
where the time goes in v2:
time: 159 us; the launch traced here: 158 us
  blocking collectives  67.7 us (43%)
  matrix products  32.5 us (20%)
  waiting for transfers between devices  23.2 us (15%)
  between operations  14.1 us (9%)
  loops' own time  10.4 us (7%)
  other arithmetic  8.14 us (5%)
  local copies, waits for them, and re-layouts  2.45 us (2%)
    all_gather x1, blocking collectives, shards(): gram = lax.all_gather(partial_gram, ('task', 'param')).sum(axis=0)  67.7 us
    all_gather x1, waiting for transfers between devices, shards(): everyone = lax.all_gather(out_grads, 'task', axis=0, tiled=True)  22.5 us
    dot_general x1, matrix products, shards(): partial_gram = jnp.dot(flat, flat.T, preferred_element_type=jnp.float32)  20.1 us
    another operation x1, loops' own time, pcgrad_weights(): mix = lax.fori_loop(0, count, turn, jnp.eye(count, dtype=jnp.float32))  10.4 us
    reduce_sum x4, other arithmetic, turn(): scale = jnp.sum(column * onehot) + 1e-06  5.13 us
    dot_general x1, matrix products, task_grads(): jnp.einsum('td,ktc->kdc', acts_part, blocks, preferred_element_type=jnp.f...  3.88 us
  transfers between devices with their start and end apart: 1, of which 1 were waited for; matrix products, arithmetic and copies ran while one was open for 0% of the time, Pallas kernels for 0%

profile of v2, /device:TPU:0, one launch (start us, length us, event | category | flops | bytes accessed | tf_op | source)
XLA Modules:
  0.0 158.5 jit_solution(10263161753390968753)
XLA Ops:
  7.2 0.7 all-gather.4.cloned.1.call-update
  7.9 22.5 %all-gather.4.cloned.1.call-done = bf16[4,128,1280]{2,1,0:T(8,128)(2,1)} async-done(((bf16[1,128,1280]{2,1,0:T(8,128)(2,1)}), bf16[4,128,1280]{2,1,0:T(8,128)(2,1)}) %all-gather.4.cloned.1.call-update) | async-done | bytes 1310736 | tf_op jit(solution)/shard_map/all_gather | solution.py:37
  30.5 3.9 %convolution_convert_fusion = bf16[896,4,1280]{2,0,1:T(8,128)(2,1)S(1)} fusion(bf16[4,128,1280]{2,1,0:T(8,128)(2,1)} %all-gather.4.cloned.1.call-done, bf16[128,3584]{1,0:T(8,128)(2,1)S(1)} %copy-done, s32[]{:T(128)S(6)} %select_n.15), kind=kOutput, calls=%fused_computation.10 | convolution fusion | flops 1178992640 | bytes 10715140 | tf_op jit(solution)/shard_map/td,ktc->kdc/dot_general | solution.py:8
  34.4 20.1 %fusion.9 = f32[1,4,4]{2,1,0:T(4,128)S(1)} fusion(bf16[896,4,1280]{2,0,1:T(8,128)(2,1)S(1)} %convolution_convert_fusion), kind=kOutput, calls=%fused_computation.15 | convolution fusion | flops 36700160 | bytes 9175104 | tf_op jit(solution)/shard_map/dot_general | solution.py:40
  54.4 67.7 %all-gather.1 = f32[32,4,4]{2,1,0:T(4,128)S(1)} all-gather(f32[1,4,4]{2,1,0:T(4,128)S(1)} %fusion.9), channel_id=2, replica_groups=mesh['task'=4,'param'=8] {'task','param'}, dimensions={0}, use_global_device_ids=true | all-gather | bytes 2112 | tf_op jit(solution)/shard_map/all_gather | solution.py:41
  122.3 23.9 %while.14 = (s32[]{:T(128)}, f32[4,4]{1,0:T(4,128)S(1)}, s32[4]{0:T(128)S(1)}, f32[4,4]{0,1:T(4,128)S(1)}, s32[]{:T(128)}, /*index=5*/s32[]{:T(128)}, s32[]{:T(128)}, f32[]{:T(128)}) while((s32[]{:T(128)}, f32[4,4]{1,0:T(4,128)S(1)}, s32[4]{0:T(128)S(1)}, f32[4,4]{0,1:T(4,128)S(1)}, s32[]{:T(128)}, /*index=5*/s32[]{:T(128)}, ...), condition=%wide.region_3.0_spmd.clone, body=%wide.region_1.0_spmd.clone.sunk | while | flops 273 | bytes 2939 | solution.py:26
  122.3 0.6 dynamic_slice.35
  124.8 1.3 fusion.24
  126.7 0.8 fusion.25
  127.5 0.7 compare_convert_fusion.2
  128.2 0.6 dynamic_slice.35
  130.8 1.3 fusion.24
  132.7 0.8 fusion.25
  133.5 0.7 compare_convert_fusion.2
  134.2 0.6 dynamic_slice.35
  136.7 1.3 fusion.24
  138.6 0.8 fusion.25
  139.4 0.7 compare_convert_fusion.2
  140.2 0.6 dynamic_slice.35
  142.7 1.3 fusion.24
  144.6 0.8 fusion.25
  145.4 0.7 compare_convert_fusion.2
  146.2 2.5 %fusion.7 = bf16[1,128,1280]{2,0,1:T(2,128)(2,1)S(1)} fusion(bf16[4,128,1280]{2,1,0:T(8,128)(2,1)S(1)} %copy-done.1, f32[4]{0:T(128)S(1)} %reduce_sum.32), kind=kOutput, calls=%fused_computation.13 | convolution fusion | flops 7864320 | bytes 1638416 | tf_op jit(solution)/shard_map/k,ktc->tc/dot_general | solution.py:43
  148.7 2.9 %fusion.10 = f32[896,1280]{1,0:T(8,128)} fusion(bf16[1,128,1280]{2,0,1:T(2,128)(2,1)S(1)} %fusion.7, bf16[128,3584]{1,0:T(8,128)(2,1)S(1)} %copy-done, s32[]{:T(128)S(6)} %select_n.15), kind=kOutput, calls=%fused_computation.17 | convolution fusion | flops 293601280 | bytes 5472260 | tf_op jit(solution)/shard_map/dot_general | solution.py:46
  (17 shorter events, 0.5 us)
Async XLA Ops:
  7.2 23.3 %copy-start = (bf16[128,3584]{1,0:T(8,128)(2,1)S(1)}, bf16[128,3584]{1,0:T(8,128)(2,1)}, u32[]{:S(2)}) copy-start(bf16[128,3584]{1,0:T(8,128)(2,1)} %param.5) | copy-start | bytes 2752516
  7.2 23.3 %all-gather.4.cloned.1.call-start = ((), (), s32[]{:S(2)}) async-start(), calls=%async_computation | async-start | bytes 1638400 | tf_op jit(solution)/shard_map/all_gather | solution.py:37
  34.4 87.9 %copy-start.3 = (s32[4]{0:T(128)S(1)}, s32[4]{0:T(128)}, u32[]{:S(2)}) copy-start(s32[4]{0:T(128)} %param.7) | copy-start | bytes 52
  34.4 111.8 %copy-start.1 = (bf16[4,128,1280]{2,1,0:T(8,128)(2,1)S(1)}, bf16[4,128,1280]{2,1,0:T(8,128)(2,1)}, u32[]{:S(2)}) copy-start(bf16[4,128,1280]{2,1,0:T(8,128)(2,1)} %all-gather.4.cloned.1.call-done) | copy-start | bytes 3932164
  146.2 5.5 %copy-start.2 = (f32[4]{0:T(128)}, f32[4]{0:T(128)S(1)}, u32[]{:S(2)}) copy-start(f32[4]{0:T(128)S(1)} %reduce_sum.32) | copy-start | bytes 52
Sparse Core Ops, SparseCore 0:
  9.5 20.8 all-gather.3
